TPU v7x, 128 devices: a whole 4x4x4 slice. The times are simulated.
128 devices in a mesh: dp: 1, tp: 16 (over z, y), sp: 8 (over x, core).
Axes of the slice: x: 4, y: 4, z: 4, core: 2. Of those that a mesh axis runs over, the one named last changes fastest.
Arguments:
- x_tokens: bfloat16 [8192, 4096], P(('dp', 'sp'), 'tp')
- doc_ids: int32 [8192], P(('dp', 'sp'))
- w_qkv: bfloat16 [4096, 12288], P('sp', 'tp')
- w_out: bfloat16 [4096, 4096], P('sp', 'tp')
Outputs:
- output: bfloat16 [8192, 4096], P(('dp', 'sp', 'tp'))
All inputs are finite; a program needn't handle non-finite values.
Results may differ from a plain program's by a relative error of at most 0.00246272.
Values are sent between devices in bfloat16 or wider.
A program may use at most 1 GiB of HBM per device.

v0:
```python
import jax
import jax.numpy as jnp
from jax import lax
from jax.sharding import PartitionSpec as P

HEAD_DIM = 128
SOFTMAX_SCALE = HEAD_DIM ** -0.5


def solution(mesh):
    def device_block(x_block, doc_block, wqkv_block, wout_block):
        x_rows = lax.all_gather(x_block, "tp", axis=1, tiled=True)
        wqkv_cols = lax.all_gather(wqkv_block, "sp", axis=0, tiled=True)
        qkv_local = jnp.dot(x_rows, wqkv_cols, preferred_element_type=jnp.float32).astype(jnp.bfloat16)
        row_count = x_rows.shape[0]
        head_count = wqkv_cols.shape[1] // (3 * HEAD_DIM)
        qkv_local = qkv_local.reshape(row_count, head_count, 3, HEAD_DIM)
        query_loc = qkv_local[:, :, 0]
        kv_all = lax.all_gather(qkv_local[:, :, 1:], "sp", axis=0, tiled=True)
        doc_all = lax.all_gather(doc_block, "sp", axis=0, tiled=True)
        scores = jnp.einsum("qhd,khd->hqk", query_loc, kv_all[:, :, 0], preferred_element_type=jnp.float32) * SOFTMAX_SCALE
        same_doc = doc_block[:, None] == doc_all[None, :]
        scores = jnp.where(same_doc[None], scores, -jnp.inf)
        weights = jax.nn.softmax(scores, axis=-1).astype(jnp.bfloat16)
        context = jnp.einsum("hqk,khd->qhd", weights, kv_all[:, :, 1], preferred_element_type=jnp.float32).astype(jnp.bfloat16)
        context = context.reshape(row_count, head_count * HEAD_DIM)
        ctx_rows = lax.all_gather(context, "tp", axis=1, tiled=True)
        wout_cols = lax.all_gather(wout_block, "sp", axis=0, tiled=True)
        y_block = jnp.dot(ctx_rows, wout_cols, preferred_element_type=jnp.float32).astype(jnp.bfloat16)
        return lax.all_to_all(y_block, "tp", 0, 1, tiled=True)

    return jax.shard_map(
        device_block,
        mesh=mesh,
        in_specs=(P(("dp", "sp"), "tp"), P(("dp", "sp")), P("sp", "tp"), P("sp", "tp")),
        out_specs=P(("dp", "sp", "tp"), None),
        check_vma=False,
    )
```

profile of v0, /device:TPU:0, one launch (start us, length us, event | category | flops | bytes accessed | tf_op | source)
XLA Modules:
  0.0 420.6 jit_solution(8849848910542667915)
XLA Ops:
  6.5 0.0 all-gather.8.cloned.1.call-start
  6.5 0.7 all-gather.8.cloned.1.call-update
  7.3 0.0 all-gather.6.cloned.1.call-start
  7.3 0.7 all-gather.6.cloned.1.call-update
  8.0 0.0 copy-start
  8.0 0.0 all-gather.10.cloned.1.call-start
  8.1 44.0 %all-gather.8.cloned.1.call-done = bf16[4096,768]{1,0:T(8,128)(2,1)} async-done(((bf16[512,768]{1,0:T(8,128)(2,1)}), bf16[4096,768]{1,0:T(8,128)(2,1)}) %all-gather.8.cloned.1.call-update) | async-done | bytes 6291472 | tf_op jit(solution)/shard_map/all_gather | solution.py:13
  52.1 78.9 %all-gather.6.cloned.1.call-done = bf16[1024,4096]{1,0:T(8,128)(2,1)} async-done(((bf16[1024,256]{1,0:T(8,128)(2,1)}), bf16[1024,4096]{1,0:T(8,128)(2,1)}) %all-gather.6.cloned.1.call-update) | async-done | bytes 8388624 | tf_op jit(solution)/shard_map/all_gather | solution.py:12
  131.0 11.0 %convolution_convert_fusion = bf16[1024,768]{0,1:T(8,128)(2,1)S(1)} fusion(bf16[1024,4096]{1,0:T(8,128)(2,1)} %all-gather.6.cloned.1.call-done, bf16[4096,768]{1,0:T(8,128)(2,1)} %all-gather.8.cloned.1.call-done), kind=kOutput, calls=%fused_computation.13 | convolution fusion | flops 6443237376 | bytes 16252928 | tf_op jit(solution)/shard_map/dot_general | solution.py:14
  142.0 0.1 slice.16
  142.1 1.3 copy.14
  143.4 0.0 all-gather.10.cloned.1.call-update
  143.4 0.0 all-gather.14.cloned.1.call-start
  143.4 0.5 all-gather.14.cloned.1.call-update
  144.0 0.0 all-gather.12.cloned.1.call-start
  144.0 0.0 copy-done
  144.0 13.0 %all_gather.21 = s32[8192]{0:T(1024)S(1)} all-gather(s32[1024]{0:T(1024)S(1)} %copy-done), channel_id=1, replica_groups=mesh['dp'=1,'tp'=16,'sp'=8] {'sp'}, dimensions={0}, use_global_device_ids=true | all-gather | bytes 36864 | tf_op jit(solution)/shard_map/all_gather | solution.py:20
  157.0 8.7 %broadcast_compare_fusion = pred[1024,8192]{1,0:T(8,128)(4,1)} fusion(s32[8192]{0:T(1024)S(1)} %all_gather.21, s32[1024]{0:T(1024)S(1)} %copy-done), kind=kLoop, calls=%fused_computation.9 | loop fusion | flops 8388608 | bytes 8425472 | tf_op jit(solution)/shard_map/eq | solution.py:22
  165.7 26.5 %all-gather.10.cloned.1.call-done = bf16[8192,2,2,128]{3,0,1,2:T(8,128)(2,1)} async-done(((bf16[1024,2,2,128]{3,0,1,2:T(8,128)(2,1)}), bf16[8192,2,2,128]{3,0,1,2:T(8,128)(2,1)}) %all-gather.10.cloned.1.call-update) | async-done | bytes 8388624 | tf_op jit(solution)/shard_map/all_gather | solution.py:19
  192.2 25.3 %fusion.6 = f32[2,1024,8192]{2,1,0:T(8,128)} fusion(bf16[8192,2,2,128]{3,0,1,2:T(8,128)(2,1)} %all-gather.10.cloned.1.call-done, bf16[1024,2,3,128]{0,3,2,1:T(8,128)(2,1)S(1)} %bitcast.27), kind=kOutput, calls=%fused_computation.11 | convolution fusion | flops 4294967296 | bytes 71827456 | tf_op jit(solution)/shard_map/qhd,khd->hqk/dot_general | solution.py:21
  217.5 76.5 %fusion.10 = (f32[2,1024]{1,0:T(2,128)S(1)}, f32[2,1024,8192]{2,1,0:T(8,128)}) fusion(f32[2,1024,8192]{2,1,0:T(8,128)} %fusion.6, pred[1024,8192]{1,0:T(8,128)(4,1)} %broadcast_compare_fusion), kind=kOutput, calls=%fused_computation.19 | output fusion | flops 100671488 | bytes 142614528 | tf_op jit(solution)/shard_map/sub | solution.py:24
  294.0 25.4 %fusion.7 = bf16[2,128,1024]{2,1,0:T(8,128)(2,1)} fusion(f32[2,1024,8192]{2,1,0:T(8,128)} %get-tuple-element.6, f32[2,1024]{1,0:T(2,128)S(1)} %get-tuple-element.5, bf16[8192,2,2,128]{3,0,1,2:T(8,128)(2,1)} %all-gather.10.cloned.1.call-done), kind=kOutput, calls=%fused_computation.15 | convolution fusion | flops 4328783872 | bytes 71835648 | tf_op jit(solution)/shard_map/hqk,khd->qhd/dot_general | solution.py:25
  319.4 0.0 all-gather.12.cloned.1.call-update
  319.4 0.0 all-gather.14.cloned.1.call-done
  319.4 71.1 %all-gather.12.cloned.1.call-done = bf16[1024,4096]{0,1:T(8,128)(2,1)} async-done(((bf16[1024,256]{0,1:T(8,128)(2,1)}), bf16[1024,4096]{0,1:T(8,128)(2,1)}) %all-gather.12.cloned.1.call-update) | async-done | bytes 8388624 | tf_op jit(solution)/shard_map/all_gather | solution.py:27
  390.6 6.4 %convolution_convert_fusion.1 = bf16[1024,256]{1,0:T(8,128)(2,1)S(1)} fusion(bf16[1024,4096]{0,1:T(8,128)(2,1)} %all-gather.12.cloned.1.call-done, bf16[4096,256]{1,0:T(8,128)(2,1)} %all-gather.14.cloned.1.call-done), kind=kOutput, calls=%fused_computation.14 | convolution fusion | flops 2147745792 | bytes 11010048 | tf_op jit(solution)/shard_map/dot_general | solution.py:29
  397.0 16.3 %all_to_all.19 = bf16[16,64,256]{2,1,0:T(8,128)(2,1)S(1)} all-to-all(bf16[16,64,256]{2,1,0:T(8,128)(2,1)S(1)} %bitcast.25), channel_id=1, replica_groups=mesh['dp'=1,'tp'=16,'sp'=8] {'tp'}, dimensions={0} | all-to-all | bytes 1048576 | tf_op jit(solution)/shard_map/all_to_all | solution.py:30
  413.3 0.8 copy.16
Async XLA Ops:
  6.5 45.6 %all-gather.8.cloned.1.call-start = ((), (), s32[]{:S(2)}) async-start(), calls=%async_computation.2 | async-start | bytes 7077888 | tf_op jit(solution)/shard_map/all_gather | solution.py:13
  7.3 123.7 %all-gather.6.cloned.1.call-start = ((), (), s32[]{:S(2)}) async-start(), calls=%async_computation.1 | async-start | bytes 8912896 | tf_op jit(solution)/shard_map/all_gather | solution.py:12
  8.0 136.0 %copy-start = (s32[1024]{0:T(1024)S(1)}, s32[1024]{0:T(1024)}, u32[]{:S(2)}) copy-start(s32[1024]{0:T(1024)} %param.5) | copy-start | bytes 12292
  8.0 184.2 %all-gather.10.cloned.1.call-start = ((), (), s32[]{:S(2)}) async-start(), calls=%async_computation.3 | async-start | bytes 9437184 | tf_op jit(solution)/shard_map/all_gather | solution.py:19
  143.4 176.1 %all-gather.14.cloned.1.call-start = ((), (), s32[]{:S(2)}) async-start(), calls=%async_computation.5 | async-start | bytes 2359296 | tf_op jit(solution)/shard_map/all_gather | solution.py:28
  144.0 246.6 %all-gather.12.cloned.1.call-start = ((), (), s32[]{:S(2)}) async-start(), calls=%async_computation.4 | async-start | bytes 8912896 | tf_op jit(solution)/shard_map/all_gather | solution.py:27
Sparse Core Ops, SparseCore 0:
  9.0 43.0 all-gather.7
  54.2 76.7 all-gather.5
  143.5 48.6 all-gather.9
  193.8 25.2 all-gather.13
  319.5 71.0 all-gather.11
where the time goes:
time: 421 us
  waiting for transfers between devices  223 us (53%)
  other arithmetic  85.2 us (20%)
  matrix products  68 us (16%)
  blocking collectives  29.4 us (7%)
  between operations  13.2 us (3%)
    all_gather x1, waiting for transfers between devices, device_block(): x_rows = lax.all_gather(x_block, 'tp', axis=1, tiled=True)  78.9 us
    sub x1, other arithmetic, device_block(): weights = jax.nn.softmax(scores, axis=-1).astype(jnp.bfloat16)  76.5 us
    all_gather x1, waiting for transfers between devices, device_block(): ctx_rows = lax.all_gather(context, 'tp', axis=1, tiled=True)  71.1 us
    all_gather x1, waiting for transfers between devices, device_block(): wqkv_cols = lax.all_gather(wqkv_block, 'sp', axis=0, tiled=True)  44 us
    all_gather x1, waiting for transfers between devices, device_block(): kv_all = lax.all_gather(qkv_local[:, :, 1:], 'sp', axis=0, tiled=True)  26.5 us
    dot_general x1, matrix products, device_block(): jnp.einsum('hqk,khd->qhd', weights, kv_all[:, :, 1], preferred_element_ty...  25.4 us
    dot_general x1, matrix products, device_block(): jnp.einsum('qhd,khd->hqk', query_loc, kv_all[:, :, 0], preferred_element_...  25.3 us
    all_to_all x1, blocking collectives, device_block(): return lax.all_to_all(y_block, 'tp', 0, 1, tiled=True)  16.3 us
  transfers between devices with their start and end apart: 5, of which 4 were waited for; matrix products, arithmetic and copies ran while one was open for 32% of the time, Pallas kernels for 0%

commit v1 on v0

v1 whole, which is shorter than its diff:
```python
import functools

import jax
import jax.numpy as jnp
from jax import lax
from jax.experimental import pallas as pl
from jax.experimental.pallas import tpu as pltpu
from jax.sharding import PartitionSpec as P

HEAD_DIM = 128
EXP2_SCALE = HEAD_DIM ** -0.5 * 1.4426950408889634
FLOOR = -3.0e38


def attention_kernel(qb, kb, sub, q_ref, kv_ref, segq_ref, segk_ref, segall_ref, o_ref, acc_ref, m_ref, l_ref):
    segq_row = segq_ref[0]
    lo = jnp.min(segq_row)
    hi = jnp.max(segq_row)
    seg_all = segall_ref[...]
    first = jnp.sum(jnp.where(seg_all < lo, 1.0, 0.0)).astype(jnp.int32)
    last = jnp.sum(jnp.where(seg_all <= hi, 1.0, 0.0)).astype(jnp.int32)
    one_doc = lo == hi

    acc_ref[...] = jnp.zeros_like(acc_ref)
    l_ref[...] = jnp.zeros_like(l_ref)
    m_ref[...] = jnp.full_like(m_ref, FLOOR)

    def block(j, masked):
        start = pl.multiple_of(j * kb, kb)
        k = kv_ref[pl.ds(start, kb), :HEAD_DIM]
        v = kv_ref[pl.ds(start, kb), HEAD_DIM:]
        if masked:
            segk_row = segk_ref[j]
        for i in range(qb // sub):
            rows = slice(i * sub, (i + 1) * sub)
            s = lax.dot_general(q_ref[rows, :], k, (((1,), (1,)), ((), ())), preferred_element_type=jnp.float32)
            t = s * EXP2_SCALE
            if masked:
                segq_col = jnp.broadcast_to(segq_row[:, rows], (HEAD_DIM, sub)).T
                t = jnp.where(segq_col[:, :1] == segk_row, t, -jnp.inf)
            m_prev = m_ref[rows, :1]
            m_new = jnp.maximum(m_prev, jnp.max(t, axis=1, keepdims=True))
            p = jnp.exp2(t - m_new)
            alpha = jnp.exp2(m_prev - m_new)
            l_new = l_ref[rows, :1] * alpha + jnp.sum(p, axis=1, keepdims=True)
            pv = jnp.dot(p.astype(jnp.bfloat16), v, preferred_element_type=jnp.float32)
            acc_ref[rows, :] = acc_ref[rows, :] * alpha + pv
            m_ref[rows, :] = jnp.broadcast_to(m_new, (sub, HEAD_DIM))
            l_ref[rows, :] = jnp.broadcast_to(l_new, (sub, HEAD_DIM))

    def step(j, carry):
        whole = one_doc & (j * kb >= first) & ((j + 1) * kb <= last)

        @pl.when(whole)
        def _():
            block(j, False)

        @pl.when(jnp.logical_not(whole))
        def _():
            block(j, True)

        return carry

    lax.fori_loop(first // kb, (last + kb - 1) // kb, step, 0)
    o_ref[...] = (acc_ref[...] / l_ref[...]).astype(o_ref.dtype)


def attention(q, kv, seg_q, seg_all, qb=512, kb=512, sub=256):
    rows, keys = q.shape[0], kv.shape[0]
    heads = q.shape[1] // HEAD_DIM
    return pl.pallas_call(
        functools.partial(attention_kernel, qb, kb, sub),
        grid=(heads, rows // qb),
        out_shape=jax.ShapeDtypeStruct(q.shape, jnp.bfloat16),
        in_specs=[
            pl.BlockSpec((qb, HEAD_DIM), lambda h, i: (i, h)),
            pl.BlockSpec((keys, 2 * HEAD_DIM), lambda h, i: (0, h)),
            pl.BlockSpec((1, 1, qb), lambda h, i: (i, 0, 0)),
            pl.BlockSpec((keys // kb, 1, kb), lambda h, i: (0, 0, 0)),
            pl.BlockSpec((keys // HEAD_DIM, HEAD_DIM), lambda h, i: (0, 0)),
        ],
        out_specs=pl.BlockSpec((qb, HEAD_DIM), lambda h, i: (i, h)),
        scratch_shapes=[
            pltpu.VMEM((qb, HEAD_DIM), jnp.float32),
            pltpu.VMEM((qb, HEAD_DIM), jnp.float32),
            pltpu.VMEM((qb, HEAD_DIM), jnp.float32),
        ],
        compiler_params=pltpu.CompilerParams(vmem_limit_bytes=48 * 1024 * 1024),
        name="attention",
    )(q, kv, seg_q.reshape(rows // qb, 1, qb), seg_all.reshape(keys // kb, 1, kb), seg_all.reshape(keys // HEAD_DIM, HEAD_DIM))


def solution(mesh):
    def device_block(x_block, doc_block, wqkv_block, wout_block):
        x_rows = lax.all_gather(x_block, "tp", axis=1, tiled=True)
        wqkv_cols = lax.all_gather(wqkv_block, "sp", axis=0, tiled=True)
        qkv_local = jnp.dot(x_rows, wqkv_cols, preferred_element_type=jnp.float32).astype(jnp.bfloat16)
        row_count = x_rows.shape[0]
        head_count = wqkv_cols.shape[1] // (3 * HEAD_DIM)
        qkv_local = qkv_local.reshape(row_count, head_count, 3 * HEAD_DIM)
        query_loc = qkv_local[:, :, :HEAD_DIM].reshape(row_count, head_count * HEAD_DIM)
        kv_loc = qkv_local[:, :, HEAD_DIM:].reshape(row_count, head_count * 2 * HEAD_DIM)
        kv_all = lax.all_gather(kv_loc, "sp", axis=0, tiled=True)
        doc_all = lax.all_gather(doc_block, "sp", axis=0, tiled=True)
        context = attention(query_loc, kv_all, doc_block, doc_all)
        ctx_rows = lax.all_gather(context, "tp", axis=1, tiled=True)
        wout_cols = lax.all_gather(wout_block, "sp", axis=0, tiled=True)
        y_block = jnp.dot(ctx_rows, wout_cols, preferred_element_type=jnp.float32).astype(jnp.bfloat16)
        return lax.all_to_all(y_block, "tp", 0, 1, tiled=True)

    return jax.shard_map(
        device_block,
        mesh=mesh,
        in_specs=(P(("dp", "sp"), "tp"), P(("dp", "sp")), P("sp", "tp"), P("sp", "tp")),
        out_specs=P(("dp", "sp", "tp"), None),
        check_vma=False,
    )
```

time: 421 us -> 347 us (0.82)
  other arithmetic: 85.2 us -> 0 us
  matrix products: 68 us -> 17.3 us
  waiting for transfers between devices: 223 us -> 257 us
  Pallas kernels: 0 us -> 25.2 us
    sub x1 -> x0, other arithmetic: 76.5 us -> none  [device_block(): weights = jax.nn.softmax(scores, axis=-1).astype(jnp.bfloat16)]
    dot_general x2 -> x0, matrix products: 50.7 us -> none  [the longest x1 25.4 us: device_block(): jnp.einsum('hqk,khd->qhd', weights, kv_all[:, :, 1], preferred_element_ty...]
    pallas_call x0 -> x1, Pallas kernels: none -> 25.2 us  [attention(): pl.pallas_call(functools.partial(attention_kernel, qb, kb, sub), grid=(he...]
    all_gather x1, waiting for transfers between devices: 71.1 us -> 95.1 us  [device_block(): ctx_rows = lax.all_gather(context, 'tp', axis=1, tiled=True)]
    eq x1 -> x0, other arithmetic: 8.7 us -> none  [device_block(): same_doc = doc_block[:, None] == doc_all[None, :]]
    all_gather x1, waiting for transfers between devices: 26.5 us -> 34.9 us  [device_block(): kv_all = lax.all_gather(kv_loc, 'sp', axis=0, tiled=True)]
  transfers between devices with their start and end apart: 5 -> 5, of which waited for: 4 -> 5; matrix products, arithmetic and copies ran while one was open for 32% -> 0% of each run, Pallas kernels for 0% -> 7%
where the time goes in v1:
time: 347 us; the launch traced here: 343 us
  waiting for transfers between devices  257 us (74%)
  blocking collectives  27.9 us (8%)
  Pallas kernels  25.2 us (7%)
  matrix products  17.3 us (5%)
  between operations  13.2 us (4%)
    all_gather x1, waiting for transfers between devices, device_block(): ctx_rows = lax.all_gather(context, 'tp', axis=1, tiled=True)  95.1 us
    all_gather x1, waiting for transfers between devices, device_block(): x_rows = lax.all_gather(x_block, 'tp', axis=1, tiled=True)  78.9 us
    all_gather x1, waiting for transfers between devices, device_block(): wqkv_cols = lax.all_gather(wqkv_block, 'sp', axis=0, tiled=True)  44 us
    all_gather x1, waiting for transfers between devices, device_block(): kv_all = lax.all_gather(kv_loc, 'sp', axis=0, tiled=True)  34.9 us
    pallas_call x1, Pallas kernels, attention(): pl.pallas_call(functools.partial(attention_kernel, qb, kb, sub), grid=(he...  25.2 us
    all_to_all x1, blocking collectives, device_block(): return lax.all_to_all(y_block, 'tp', 0, 1, tiled=True)  14.8 us
    all_gather x1, blocking collectives, device_block(): doc_all = lax.all_gather(doc_block, 'sp', axis=0, tiled=True)  13 us
    dot_general x1, matrix products, device_block(): jnp.dot(x_rows, wqkv_cols, preferred_element_type=jnp.float32)  11 us
  transfers between devices with their start and end apart: 5, of which 5 were waited for; matrix products, arithmetic and copies ran while one was open for 0% of the time, Pallas kernels for 7%

profile of v1, /device:TPU:0, one launch (start us, length us, event | category | flops | bytes accessed | tf_op | source)
XLA Modules:
  0.0 342.7 jit_solution(13522929386741856384)
XLA Ops:
  6.5 0.0 all-gather.8.cloned.1.call-start
  6.5 0.7 all-gather.8.cloned.1.call-update
  7.3 0.0 all-gather.6.cloned.1.call-start
  7.3 0.7 all-gather.6.cloned.1.call-update
  8.0 0.0 copy-start
  8.0 0.0 all-gather.10.cloned.1.call-start
  8.1 44.0 %all-gather.8.cloned.1.call-done = bf16[4096,768]{1,0:T(8,128)(2,1)} async-done(((bf16[512,768]{1,0:T(8,128)(2,1)}), bf16[4096,768]{1,0:T(8,128)(2,1)}) %all-gather.8.cloned.1.call-update) | async-done | bytes 6291472 | tf_op jit(solution)/shard_map/all_gather | solution.py:96
  52.1 78.9 %all-gather.6.cloned.1.call-done = bf16[1024,4096]{1,0:T(8,128)(2,1)} async-done(((bf16[1024,256]{1,0:T(8,128)(2,1)}), bf16[1024,4096]{1,0:T(8,128)(2,1)}) %all-gather.6.cloned.1.call-update) | async-done | bytes 8388624 | tf_op jit(solution)/shard_map/all_gather | solution.py:95
  131.0 11.0 %convolution_convert_fusion = bf16[1024,768]{0,1:T(8,128)(2,1)S(1)} fusion(bf16[1024,4096]{1,0:T(8,128)(2,1)} %all-gather.6.cloned.1.call-done, bf16[4096,768]{1,0:T(8,128)(2,1)} %all-gather.8.cloned.1.call-done), kind=kOutput, calls=%fused_computation | convolution fusion | flops 6443237376 | bytes 16252928 | tf_op jit(solution)/shard_map/dot_general | solution.py:97
  142.0 0.1 slice.9
  142.1 1.3 copy.14
  143.4 0.0 all-gather.10.cloned.1.call-update
  143.4 0.0 all-gather.14.cloned.1.call-start
  143.5 0.5 all-gather.14.cloned.1.call-update
  144.0 0.0 all-gather.12.cloned.1.call-start
  144.0 0.0 copy-done
  144.0 13.0 %all_gather.21 = s32[8192]{0:T(1024)S(1)} all-gather(s32[1024]{0:T(1024)S(1)} %copy-done), channel_id=1, replica_groups=mesh['dp'=1,'tp'=16,'sp'=8] {'sp'}, dimensions={0}, use_global_device_ids=true | all-gather | bytes 36864 | tf_op jit(solution)/shard_map/all_gather | solution.py:104
  157.1 0.2 copy.13.q_ref
  157.3 34.9 %all-gather.10.cloned.1.call-done.kv_ref = bf16[8192,512]{1,0:T(8,128)(2,1)} async-done(((bf16[1024,512]{1,0:T(8,128)(2,1)}), bf16[8192,512]{1,0:T(8,128)(2,1)}) %all-gather.10.cloned.1.call-update) | async-done | bytes 8388624 | tf_op jit(solution)/shard_map/all_gather | solution.py:103
  192.2 25.2 %attention.1 = bf16[1024,256]{1,0:T(8,128)(2,1)} custom-call(bf16[1024,256]{1,0:T(8,128)(2,1)S(1)} %copy.13.q_ref, bf16[8192,512]{1,0:T(8,128)(2,1)} %all-gather.10.cloned.1.call-done.kv_ref, s32[2,1,512]{2,1,0:T(1,128)S(1)} %bitcast.16, s32[16,1,512]{2,1,0:T(1,128)S(1)} %bitcast.14, s32[64,128]{1,0:T(8,128)S(1)} %bitcast.15), custom_call_target="tpu_custom_call" | custom-call | tf_op jit(solution)/shard_map/attention/pallas_call | solution.py:71
  217.4 0.0 all-gather.12.cloned.1.call-update
  217.4 1.7 all-gather.14.cloned.1.call-done
  219.1 95.1 %all-gather.12.cloned.1.call-done = bf16[1024,4096]{1,0:T(8,128)(2,1)} async-done(((bf16[1024,256]{1,0:T(8,128)(2,1)}), bf16[1024,4096]{1,0:T(8,128)(2,1)}) %all-gather.12.cloned.1.call-update) | async-done | bytes 8388624 | tf_op jit(solution)/shard_map/all_gather | solution.py:106
  314.2 6.3 %convolution_convert_fusion.1 = bf16[1024,256]{1,0:T(8,128)(2,1)S(1)} fusion(bf16[1024,4096]{1,0:T(8,128)(2,1)} %all-gather.12.cloned.1.call-done, bf16[4096,256]{1,0:T(8,128)(2,1)} %all-gather.14.cloned.1.call-done), kind=kOutput, calls=%fused_computation.1 | convolution fusion | flops 2147745792 | bytes 11010048 | tf_op jit(solution)/shard_map/dot_general | solution.py:108
  320.5 14.8 %all_to_all.19 = bf16[16,64,256]{2,1,0:T(8,128)(2,1)S(1)} all-to-all(bf16[16,64,256]{2,1,0:T(8,128)(2,1)S(1)} %bitcast.22), channel_id=1, replica_groups=mesh['dp'=1,'tp'=16,'sp'=8] {'tp'}, dimensions={0} | all-to-all | bytes 1048576 | tf_op jit(solution)/shard_map/all_to_all | solution.py:109
  335.4 0.8 copy.15
  (1 shorter events, 0.0 us)
Async XLA Ops:
  6.5 45.6 %all-gather.8.cloned.1.call-start = ((), (), s32[]{:S(2)}) async-start(), calls=%async_computation.2 | async-start | bytes 7077888 | tf_op jit(solution)/shard_map/all_gather | solution.py:96
  7.3 123.7 %all-gather.6.cloned.1.call-start = ((), (), s32[]{:S(2)}) async-start(), calls=%async_computation.1 | async-start | bytes 8912896 | tf_op jit(solution)/shard_map/all_gather | solution.py:95
  8.0 136.0 %copy-start = (s32[1024]{0:T(1024)S(1)}, s32[1024]{0:T(1024)}, u32[]{:S(2)}) copy-start(s32[1024]{0:T(1024)} %param.5) | copy-start | bytes 12292
  8.0 184.2 %all-gather.10.cloned.1.call-start = ((), (), s32[]{:S(2)}) async-start(), calls=%async_computation.3 | async-start | bytes 9437184 | tf_op jit(solution)/shard_map/all_gather | solution.py:103
  143.4 75.7 %all-gather.14.cloned.1.call-start = ((), (), s32[]{:S(2)}) async-start(), calls=%async_computation.5 | async-start | bytes 2359296 | tf_op jit(solution)/shard_map/all_gather | solution.py:107
  144.0 170.2 %all-gather.12.cloned.1.call-start = ((), (), s32[]{:S(2)}) async-start(), calls=%async_computation.4 | async-start | bytes 8912896 | tf_op jit(solution)/shard_map/all_gather | solution.py:106
Sparse Core Ops, SparseCore 0:
  9.0 43.0 all-gather.7
  54.2 76.7 all-gather.5
  143.5 48.6 all-gather.9
  193.8 25.2 all-gather.13
  221.1 93.0 all-gather.11
